TPU v7x, 8 devices: a whole 2x2x1 slice. The times are simulated.
8 devices in a mesh: prob: 2 (over z, y), feat: 4 (over x, core).
Axes of the slice: x: 2, y: 2, z: 1, core: 2. Of those that a mesh axis runs over, the one named last changes fastest.
Arguments:
- x_data: bfloat16 [4096, 784], P('prob'), parts along dimension 0
- targets: float32 [4096], P('prob'), parts along dimension 0
- w_in: float32 [2048, 784], P(('prob', 'feat')), parts along dimension 0
- w_out: float32 [2048], P(('prob', 'feat')), parts along dimension 0
- reg_weight: float32 [2], P('prob'), parts along dimension 0
- step_size: float32 [2], P('prob'), parts along dimension 0
Outputs:
- output 1: float32 [2048, 784], P(('prob', 'feat')), parts along dimension 0
- output 2: float32 [2048], P(('prob', 'feat')), parts along dimension 0
- output 3: float32 [12], P('prob'), parts along dimension 0
There are 2 independent parts. A program takes and returns all parts, laid end to end along the dimension named above; each array names one.
All inputs are finite; a program needn't handle non-finite values.
Results may differ from a plain program's by a relative error of at most 0.001.
Values are sent between devices in bfloat16 or wider.
A program may use at most 1 GiB of HBM per device.

v0:
```python
import math
import jax
import jax.numpy as jnp
from jax import lax
from jax.sharding import PartitionSpec as P

NUM_ITERS = 6
HIST_LEN = 3
FULL_PREC = lax.Precision.HIGHEST


def pair_dot_local(first, second):
    return jnp.sum(first[0] * second[0]) + jnp.sum(first[1] * second[1])


def pair_axpy(base, coef, other):
    return (base[0] + coef * other[0], base[1] + coef * other[1])


def two_loop(full_grad, hist_s, hist_y, rho_vals, gamma_scale, dot_fn):
    query_vec = full_grad
    a_coefs = {}
    for pos_idx in reversed(range(len(hist_s))):
        a_coefs[pos_idx] = rho_vals[pos_idx] * dot_fn(hist_s[pos_idx], query_vec)
        query_vec = pair_axpy(query_vec, -a_coefs[pos_idx], hist_y[pos_idx])
    result = (gamma_scale * query_vec[0], gamma_scale * query_vec[1])
    for pos_idx in range(len(hist_s)):
        b_coef = rho_vals[pos_idx] * dot_fn(hist_y[pos_idx], result)
        result = pair_axpy(result, a_coefs[pos_idx] - b_coef, hist_s[pos_idx])
    return result


def global_dot(first, second):
    return lax.psum(pair_dot_local(first, second), "feat")


def solution(mesh):
    feat_size = mesh.shape["feat"]

    def local_solve(x_loc, t_loc, win_loc, wout_loc, reg_loc, step_loc):
        num_rows = x_loc.shape[0]
        in_scale = 1.0 / math.sqrt(x_loc.shape[1])
        out_scale = 1.0 / math.sqrt(win_loc.shape[0] * feat_size)
        reg_coef = reg_loc[0]
        step_coef = step_loc[0]
        x_f32 = x_loc.astype(jnp.float32)
        params = (win_loc, wout_loc)
        prev_params = params
        prev_grad = params
        hist_s = []
        hist_y = []
        rho_vals = []
        losses = []
        for iter_idx in range(NUM_ITERS):
            pre_act = lax.dot_general(x_f32, params[0], (((1,), (1,)), ((), ())), precision=FULL_PREC) * in_scale
            hid_act = jnp.tanh(pre_act)
            part_logits = jnp.dot(hid_act, params[1], precision=FULL_PREC) * out_scale
            logits = lax.psum(part_logits, "feat")
            losses.append(jnp.mean(jax.nn.softplus(logits) - t_loc * logits))
            resid_vec = (jax.nn.sigmoid(logits) - t_loc) / num_rows
            grad_out = jnp.dot(resid_vec, hid_act, precision=FULL_PREC) * out_scale
            d_pre = resid_vec[:, None] * (params[1] * (out_scale * in_scale))[None, :] * (1.0 - hid_act * hid_act)
            grad_in = lax.dot_general(d_pre, x_f32, (((0,), (0,)), ((), ())), precision=FULL_PREC)
            full_grad = (grad_in + reg_coef * params[0], grad_out + reg_coef * params[1])
            if iter_idx == 0:
                direction = full_grad
            else:
                s_vec = pair_axpy(params, -1.0, prev_params)
                y_vec = pair_axpy(full_grad, -1.0, prev_grad)
                curv_pair = lax.psum(jnp.stack([pair_dot_local(y_vec, s_vec), pair_dot_local(y_vec, y_vec)]), "feat")
                hist_s = (hist_s + [s_vec])[-HIST_LEN:]
                hist_y = (hist_y + [y_vec])[-HIST_LEN:]
                rho_vals = (rho_vals + [1.0 / curv_pair[0]])[-HIST_LEN:]
                gamma_scale = curv_pair[0] / curv_pair[1]
                direction = two_loop(full_grad, hist_s, hist_y, rho_vals, gamma_scale, global_dot)
            prev_params = params
            prev_grad = full_grad
            params = pair_axpy(params, -step_coef, direction)
        return params[0], params[1], jnp.stack(losses)

    specs_in = (P("prob", None), P("prob"), P(("prob", "feat"), None), P(("prob", "feat")), P("prob"), P("prob"))
    specs_out = (P(("prob", "feat"), None), P(("prob", "feat")), P("prob"))
    return jax.shard_map(local_solve, mesh=mesh, in_specs=specs_in, out_specs=specs_out, check_vma=False)
```

profile of v0, /device:TPU:0, one launch (start us, length us, event | category | flops | bytes accessed | tf_op | source)
XLA Modules:
  0.0 457.2 jit_solution(12315686363982917799)
XLA Ops:
  11.5 9.4 %psum.245 = f32[2048]{0:T(1024)S(1)} all-reduce(f32[2048]{0:T(1024)S(1)} %broadcast_multiply_fusion.5), channel_id=1, replica_groups=mesh['prob'=2,'feat'=4] {'feat'}, use_global_device_ids=true, to_apply=%region_0.0 | all-reduce | flops 2048 | bytes 16384 | tf_op jit(solution)/shard_map/psum | solution.py:58
  42.5 7.7 %multiply_reduce_fusion.31 = (f32[]{:T(128)}, f32[]{:T(128)}, f32[]{:T(128)}, f32[256,784]{0,1:T(8,128)}, f32[256,784]{0,1:T(8,128)}, /*index=5*/f32[256,784]{0,1:T(8,128)}) fusion(f32[256,784]{0,1:T(8,128)} %get-tuple-element.123, f32[256,784]{0,1:T(8,128)} %copy-done.10, f32[256,784]{0,1:T(8,128)} %param.8, f32[]{:T(128)} %bitcast.110, ...), kind=kOutput, calls=%fused_computation.134 | convolution fusion | flops 4937007104 | bytes 10134544 | tf_op jit(solution)/shard_map/dot_general | solution.py:63
  55.7 6.3 %all-reduce.4 = (f32[2]{0:T(128)S(1)}, f32[]{:T(128)}) all-reduce(f32[2]{0:T(128)S(1)} %pad_maximum_fusion, f32[]{:T(128)S(6)} %add.499), channel_id=1, replica_groups=mesh['prob'=2,'feat'=4] {'feat'}, use_global_device_ids=true, to_apply=%region_6.7 | all-reduce | flops 3 | bytes 24 | tf_op jit(solution)/shard_map/psum | solution.py:70
  69.3 6.2 %psum.249 = f32[]{:T(128)} all-reduce(f32[]{:T(128)S(6)} %add.502), channel_id=1, replica_groups=mesh['prob'=2,'feat'=4] {'feat'}, use_global_device_ids=true, to_apply=%region_12.13 | all-reduce | flops 1 | bytes 8 | tf_op jit(solution)/shard_map/psum | solution.py:34
  86.0 6.9 %psum.250 = f32[2048]{0:T(1024)S(1)} all-reduce(f32[2048]{0:T(1024)S(1)} %broadcast_multiply_fusion.3), channel_id=1, replica_groups=mesh['prob'=2,'feat'=4] {'feat'}, use_global_device_ids=true, to_apply=%region_13.14 | all-reduce | flops 2048 | bytes 16384 | tf_op jit(solution)/shard_map/psum | solution.py:58
  92.9 7.7 %multiply_reduce_fusion.27 = (f32[]{:T(128)}, f32[]{:T(128)}, f32[]{:T(128)}, f32[256,784]{0,1:T(8,128)}, f32[256,784]{0,1:T(8,128)}, /*index=5*/f32[256,784]{0,1:T(8,128)}) fusion(f32[256,784]{0,1:T(8,128)} %get-tuple-element.124, f32[256,784]{0,1:T(8,128)} %copy-done.9, f32[256,784]{0,1:T(8,128)} %copy-done.10, f32[]{:T(128)} %bitcast.109, ...), kind=kOutput, calls=%fused_computation.126 | convolution fusion | flops 4937007104 | bytes 10134544 | tf_op jit(solution)/shard_map/dot_general | solution.py:63
  106.1 6.3 %all-reduce.3 = (f32[2]{0:T(128)S(1)}, f32[]{:T(128)}) all-reduce(f32[2]{0:T(128)S(1)} %pad_maximum_fusion.1, f32[]{:T(128)S(6)} %add.516), channel_id=1, replica_groups=mesh['prob'=2,'feat'=4] {'feat'}, use_global_device_ids=true, to_apply=%region_18.19 | all-reduce | flops 3 | bytes 24 | tf_op jit(solution)/shard_map/psum | solution.py:70
  119.8 6.9 %psum.253 = f32[]{:T(128)} all-reduce(f32[]{:T(128)S(6)} %add.519), channel_id=1, replica_groups=mesh['prob'=2,'feat'=4] {'feat'}, use_global_device_ids=true, to_apply=%region_24.25 | all-reduce | flops 1 | bytes 8 | tf_op jit(solution)/shard_map/psum | solution.py:34
  132.9 6.2 %psum.254 = f32[]{:T(128)} all-reduce(f32[]{:T(128)S(6)} %add.522), channel_id=1, replica_groups=mesh['prob'=2,'feat'=4] {'feat'}, use_global_device_ids=true, to_apply=%region_27.28 | all-reduce | flops 1 | bytes 8 | tf_op jit(solution)/shard_map/psum | solution.py:34
  144.5 6.4 %psum.255 = f32[]{:T(128)} all-reduce(f32[]{:T(128)S(6)} %add.525), channel_id=1, replica_groups=mesh['prob'=2,'feat'=4] {'feat'}, use_global_device_ids=true, to_apply=%region_30.31 | all-reduce | flops 1 | bytes 8 | tf_op jit(solution)/shard_map/psum | solution.py:34
  167.8 7.7 %multiply_reduce_fusion.21 = (f32[]{:T(128)}, f32[]{:T(128)}, f32[]{:T(128)}, f32[256,784]{0,1:T(8,128)}, f32[256,784]{0,1:T(8,128)}, /*index=5*/f32[256,784]{0,1:T(8,128)}) fusion(f32[256,784]{0,1:T(8,128)} %get-tuple-element.125, f32[256,784]{0,1:T(8,128)} %copy-done.11, f32[256,784]{0,1:T(8,128)} %copy-done.9, f32[]{:T(128)} %bitcast.108, ...), kind=kOutput, calls=%fused_computation.114 | convolution fusion | flops 4937007104 | bytes 10134544 | tf_op jit(solution)/shard_map/dot_general | solution.py:63
  181.0 7.1 %all-reduce.2 = (f32[2]{0:T(128)S(1)}, f32[]{:T(128)}) all-reduce(f32[2]{0:T(128)S(1)} %pad_maximum_fusion.2, f32[]{:T(128)S(6)} %add.539), channel_id=1, replica_groups=mesh['prob'=2,'feat'=4] {'feat'}, use_global_device_ids=true, to_apply=%region_36.37 | all-reduce | flops 3 | bytes 24 | tf_op jit(solution)/shard_map/psum | solution.py:70
  194.3 6.4 %psum.259 = f32[]{:T(128)} all-reduce(f32[]{:T(128)S(6)} %add.542), channel_id=1, replica_groups=mesh['prob'=2,'feat'=4] {'feat'}, use_global_device_ids=true, to_apply=%region_42.43 | all-reduce | flops 1 | bytes 8 | tf_op jit(solution)/shard_map/psum | solution.py:34
  206.8 6.5 %psum.260 = f32[]{:T(128)} all-reduce(f32[]{:T(128)S(6)} %add.545), channel_id=1, replica_groups=mesh['prob'=2,'feat'=4] {'feat'}, use_global_device_ids=true, to_apply=%region_45.46 | all-reduce | flops 1 | bytes 8 | tf_op jit(solution)/shard_map/psum | solution.py:34
  219.5 6.2 %psum.261 = f32[]{:T(128)} all-reduce(f32[]{:T(128)S(6)} %add.548), channel_id=1, replica_groups=mesh['prob'=2,'feat'=4] {'feat'}, use_global_device_ids=true, to_apply=%region_48.49 | all-reduce | flops 1 | bytes 8 | tf_op jit(solution)/shard_map/psum | solution.py:34
  232.0 6.6 %psum.262 = f32[]{:T(128)} all-reduce(f32[]{:T(128)S(6)} %add.551), channel_id=1, replica_groups=mesh['prob'=2,'feat'=4] {'feat'}, use_global_device_ids=true, to_apply=%region_51.52 | all-reduce | flops 1 | bytes 8 | tf_op jit(solution)/shard_map/psum | solution.py:34
  243.7 6.6 %psum.263 = f32[]{:T(128)} all-reduce(f32[]{:T(128)S(6)} %add.554), channel_id=1, replica_groups=mesh['prob'=2,'feat'=4] {'feat'}, use_global_device_ids=true, to_apply=%region_54.55 | all-reduce | flops 1 | bytes 8 | tf_op jit(solution)/shard_map/psum | solution.py:34
  260.9 6.7 %psum.264 = f32[2048]{0:T(1024)S(1)} all-reduce(f32[2048]{0:T(1024)S(1)} %broadcast_multiply_fusion.1), channel_id=1, replica_groups=mesh['prob'=2,'feat'=4] {'feat'}, use_global_device_ids=true, to_apply=%region_55.56 | all-reduce | flops 2048 | bytes 16384 | tf_op jit(solution)/shard_map/psum | solution.py:58
  267.7 7.8 %multiply_reduce_fusion.13 = (f32[]{:T(128)}, f32[]{:T(128)}, f32[]{:T(128)}, f32[256,784]{0,1:T(8,128)}, f32[256,784]{0,1:T(8,128)}, /*index=5*/f32[256,784]{0,1:T(8,128)}) fusion(f32[256,784]{0,1:T(8,128)} %get-tuple-element.126, f32[256,784]{0,1:T(8,128)} %copy-done.12, f32[256,784]{0,1:T(8,128)} %copy-done.11, f32[]{:T(128)} %bitcast.107, ...), kind=kOutput, calls=%fused_computation.98 | convolution fusion | flops 4937007104 | bytes 10134544 | tf_op jit(solution)/shard_map/dot_general | solution.py:63
  281.1 6.4 %all-reduce.1 = (f32[2]{0:T(128)S(1)}, f32[]{:T(128)}) all-reduce(f32[2]{0:T(128)S(1)} %pad_maximum_fusion.3, f32[]{:T(128)S(6)} %add.568), channel_id=1, replica_groups=mesh['prob'=2,'feat'=4] {'feat'}, use_global_device_ids=true, to_apply=%region_60.61 | all-reduce | flops 3 | bytes 24 | tf_op jit(solution)/shard_map/psum | solution.py:70
  293.8 6.4 %psum.267 = f32[]{:T(128)} all-reduce(f32[]{:T(128)S(6)} %add.571), channel_id=1, replica_groups=mesh['prob'=2,'feat'=4] {'feat'}, use_global_device_ids=true, to_apply=%region_66.67 | all-reduce | flops 1 | bytes 8 | tf_op jit(solution)/shard_map/psum | solution.py:34
  306.3 6.2 %psum.268 = f32[]{:T(128)} all-reduce(f32[]{:T(128)S(6)} %add.574), channel_id=1, replica_groups=mesh['prob'=2,'feat'=4] {'feat'}, use_global_device_ids=true, to_apply=%region_69.70 | all-reduce | flops 1 | bytes 8 | tf_op jit(solution)/shard_map/psum | solution.py:34
  318.4 6.9 %psum.269 = f32[]{:T(128)} all-reduce(f32[]{:T(128)S(6)} %add.577), channel_id=1, replica_groups=mesh['prob'=2,'feat'=4] {'feat'}, use_global_device_ids=true, to_apply=%region_72.73 | all-reduce | flops 1 | bytes 8 | tf_op jit(solution)/shard_map/psum | solution.py:34
  331.4 6.5 %psum.270 = f32[]{:T(128)} all-reduce(f32[]{:T(128)S(6)} %add.580), channel_id=1, replica_groups=mesh['prob'=2,'feat'=4] {'feat'}, use_global_device_ids=true, to_apply=%region_75.76 | all-reduce | flops 1 | bytes 8 | tf_op jit(solution)/shard_map/psum | solution.py:34
  342.9 6.8 %psum.271 = f32[]{:T(128)} all-reduce(f32[]{:T(128)S(6)} %add.583), channel_id=1, replica_groups=mesh['prob'=2,'feat'=4] {'feat'}, use_global_device_ids=true, to_apply=%region_78.79 | all-reduce | flops 1 | bytes 8 | tf_op jit(solution)/shard_map/psum | solution.py:34
  366.8 7.2 %multiply_reduce_fusion.5 = (f32[]{:T(128)}, f32[]{:T(128)}, f32[]{:T(128)}, f32[256,784]{0,1:T(8,128)}) fusion(f32[256,784]{0,1:T(8,128)} %copy-done.17, f32[256,784]{0,1:T(8,128)} %copy-done.12, f32[256,784]{0,1:T(8,128)} %get-tuple-element.127, f32[]{:T(128)} %bitcast.106, bf16[2048,784]{0,1:T(8,128)(2,1)S(1)} %copy-done, f32[2048,256]{1,0:T(8,128)} %copy-done.13, ...), kind=kOutput, calls=%fused_computation.82 | convolution fusion | flops 4937007104 | bytes 8528912 | tf_op jit(solution)/shard_map/dot_general | solution.py:63
  379.4 6.3 %all-reduce = (f32[2]{0:T(128)S(1)}, f32[]{:T(128)}) all-reduce(f32[2]{0:T(128)S(1)} %pad_maximum_fusion.4, f32[]{:T(128)S(6)} %add.597), channel_id=1, replica_groups=mesh['prob'=2,'feat'=4] {'feat'}, use_global_device_ids=true, to_apply=%region_84.85 | all-reduce | flops 3 | bytes 24 | tf_op jit(solution)/shard_map/psum | solution.py:70
  392.1 6.3 %psum.275 = f32[]{:T(128)} all-reduce(f32[]{:T(128)S(6)} %add.600), channel_id=1, replica_groups=mesh['prob'=2,'feat'=4] {'feat'}, use_global_device_ids=true, to_apply=%region_90.91 | all-reduce | flops 1 | bytes 8 | tf_op jit(solution)/shard_map/psum | solution.py:34
  404.6 7.1 %psum.276 = f32[]{:T(128)} all-reduce(f32[]{:T(128)S(6)} %add.603), channel_id=1, replica_groups=mesh['prob'=2,'feat'=4] {'feat'}, use_global_device_ids=true, to_apply=%region_93.94 | all-reduce | flops 1 | bytes 8 | tf_op jit(solution)/shard_map/psum | solution.py:34
  417.6 6.4 %psum.277 = f32[]{:T(128)} all-reduce(f32[]{:T(128)S(6)} %add.606), channel_id=1, replica_groups=mesh['prob'=2,'feat'=4] {'feat'}, use_global_device_ids=true, to_apply=%region_96.97 | all-reduce | flops 1 | bytes 8 | tf_op jit(solution)/shard_map/psum | solution.py:34
  430.2 6.6 %psum.278 = f32[]{:T(128)} all-reduce(f32[]{:T(128)S(6)} %add.609), channel_id=1, replica_groups=mesh['prob'=2,'feat'=4] {'feat'}, use_global_device_ids=true, to_apply=%region_99.100 | all-reduce | flops 1 | bytes 8 | tf_op jit(solution)/shard_map/psum | solution.py:34
  442.2 6.2 %psum.279 = f32[]{:T(128)} all-reduce(f32[]{:T(128)S(6)} %add.612), channel_id=1, replica_groups=mesh['prob'=2,'feat'=4] {'feat'}, use_global_device_ids=true, to_apply=%region_102.103 | all-reduce | flops 1 | bytes 8 | tf_op jit(solution)/shard_map/psum | solution.py:34
  (139 shorter events, 164.6 us)
Async XLA Ops:
  0.6 1.9 copy-start
  2.6 7.1 %copy-start.19 = (f32[256]{0:T(256)S(1)}, f32[256]{0:T(256)}, u32[]{:S(2)}) copy-start(f32[256]{0:T(256)} %param.9) | copy-start | bytes 3076
  8.3 1.4 copy-start.15
  8.3 12.6 %copy-start.18 = (f32[2048]{0:T(1024)S(1)}, f32[2048]{0:T(1024)}, u32[]{:S(2)}) copy-start(f32[2048]{0:T(1024)} %param.7) | copy-start | bytes 24580
  20.9 2.7 copy-start.16
  28.7 4.6 %copy-start.10 = (f32[256,784]{0,1:T(8,128)}, f32[256,784]{0,1:T(8,128)S(1)}, u32[]{:S(2)}) copy-start(f32[256,784]{0,1:T(8,128)S(1)} %get-tuple-element.122) | copy-start | bytes 2408452
  33.2 1.4 copy-start.7
  42.5 7.7 %copy-start.8 = (f32[2048,256]{1,0:T(8,128)S(1)}, f32[2048,256]{1,0:T(8,128)}, u32[]{:S(2)}) copy-start(f32[2048,256]{1,0:T(8,128)} %copy-done.7) | copy-start | bytes 6291460
  78.2 4.6 %copy-start.9 = (f32[256,784]{0,1:T(8,128)}, f32[256,784]{0,1:T(8,128)S(1)}, u32[]{:S(2)}) copy-start(f32[256,784]{0,1:T(8,128)S(1)} %multiply_add_fusion.26) | copy-start | bytes 2408452
  82.8 1.4 copy-start.1
  92.9 7.8 %copy-start.2 = (f32[2048,256]{1,0:T(8,128)S(1)}, f32[2048,256]{1,0:T(8,128)}, u32[]{:S(2)}) copy-start(f32[2048,256]{1,0:T(8,128)} %copy-done.1) | copy-start | bytes 6291460
  154.0 4.6 %copy-start.11 = (f32[256,784]{0,1:T(8,128)}, f32[256,784]{0,1:T(8,128)S(1)}, u32[]{:S(2)}) copy-start(f32[256,784]{0,1:T(8,128)S(1)} %multiply_add_fusion.21) | copy-start | bytes 2408452
  158.6 1.4 copy-start.3
  167.7 7.7 %copy-start.4 = (f32[2048,256]{1,0:T(8,128)S(1)}, f32[2048,256]{1,0:T(8,128)}, u32[]{:S(2)}) copy-start(f32[2048,256]{1,0:T(8,128)} %copy-done.3) | copy-start | bytes 6291460
  253.1 4.6 %copy-start.12 = (f32[256,784]{0,1:T(8,128)}, f32[256,784]{0,1:T(8,128)S(1)}, u32[]{:S(2)}) copy-start(f32[256,784]{0,1:T(8,128)S(1)} %multiply_add_fusion.14) | copy-start | bytes 2408452
  257.7 1.4 copy-start.5
  267.6 7.8 %copy-start.6 = (f32[2048,256]{1,0:T(8,128)S(1)}, f32[2048,256]{1,0:T(8,128)}, u32[]{:S(2)}) copy-start(f32[2048,256]{1,0:T(8,128)} %copy-done.5) | copy-start | bytes 6291460
  352.5 4.6 %copy-start.17 = (f32[256,784]{0,1:T(8,128)}, f32[256,784]{0,1:T(8,128)S(1)}, u32[]{:S(2)}) copy-start(f32[256,784]{0,1:T(8,128)S(1)} %multiply_add_fusion.7) | copy-start | bytes 2408452
  357.1 1.4 copy-start.13
  366.8 7.2 %copy-start.14 = (f32[2048,256]{1,0:T(8,128)S(1)}, f32[2048,256]{1,0:T(8,128)}, u32[]{:S(2)}) copy-start(f32[2048,256]{1,0:T(8,128)} %copy-done.13) | copy-start | bytes 6291460
where the time goes:
time: 464 us; the launch traced here: 457 us
  blocking collectives  197 us (42%)
  matrix products  90.1 us (19%)
  other arithmetic  82.8 us (18%)
  between operations  75.5 us (16%)
  local copies, waits for them, and re-layouts  12.1 us (3%)
    psum x19, blocking collectives, global_dot(): return lax.psum(pair_dot_local(first, second), 'feat')  124 us
    reduce_sum x43, other arithmetic, pair_dot_local(): return jnp.sum(first[0] * second[0]) + jnp.sum(first[1] * second[1])  69.5 us
    dot_general x6, matrix products, local_solve(): lax.dot_general(d_pre, x_f32, (((0,), (0,)), ((), ())), precision=FULL_PREC)  43.1 us
    psum x6, blocking collectives, local_solve(): logits = lax.psum(part_logits, 'feat')  40.6 us
    psum x5, blocking collectives, local_solve(): lax.psum(jnp.stack([pair_dot_local(y_vec, s_vec), pair_dot_local(y_vec, y...  32.4 us
    dot_general x6, matrix products, local_solve(): lax.dot_general(x_f32, params[0], (((1,), (1,)), ((), ())), precision=FUL...  28.6 us
    add x6, other arithmetic, pair_axpy(): return (base[0] + coef * other[0], base[1] + coef * other[1])  12.1 us
    dot_general x6, matrix products, local_solve(): part_logits = jnp.dot(hid_act, params[1], precision=FULL_PREC) * out_scale  11.1 us

commit v1 on v0

v1 whole, which is shorter than its diff:
```python
import functools
import math

import jax
import jax.numpy as jnp
from jax import lax
from jax.experimental import pallas as pl
from jax.experimental.pallas import tpu as pltpu
from jax.sharding import PartitionSpec as P

NUM_ITERS = 6
HIST = 3
LANES = 128
CHUNK = 512
F32 = jnp.float32
BF16 = jnp.bfloat16
NT = (((1,), (1,)), ((), ()))
NN = (((1,), (0,)), ((), ()))


def split3(val):
    hi = val.astype(BF16)
    rest = val - hi.astype(F32)
    mid = rest.astype(BF16)
    lo = (rest - mid.astype(F32)).astype(BF16)
    return hi, mid, lo


def exact_dot(parts, rhs, dims):
    out = lax.dot_general(parts[0], rhs, dims, preferred_element_type=F32)
    for part in parts[1:]:
        out = out + lax.dot_general(part, rhs, dims, preferred_element_type=F32)
    return out


def sub_sum(val):
    return jnp.sum(val, axis=0, keepdims=True)


def kernel(feat, reg_ref, step_ref, x_ref, t_ref, w_ref, w2_ref, wout_ref, w2out_ref, loss_ref,
           theta, grad, hist_s, hist_y, p_hi, p_mid, p_lo, act, w2b, d_hi, d_mid, d_lo, zbuf, dbuf,
           z_send, z_recv, d_send, d_recv):
    rows, dim = x_ref.shape
    hid = w_ref.shape[0]
    wide = theta.shape[1]
    tail = dim // LANES * LANES
    tail_n = dim - tail
    n_chunks = rows // CHUNK
    q_n = CHUNK // LANES
    in_scale = 1.0 / math.sqrt(dim)
    out_scale = 1.0 / math.sqrt(hid * feat)
    me = lax.axis_index("feat")
    parts_refs = (p_hi, p_mid, p_lo)

    barrier = pltpu.get_barrier_semaphore()
    for off in range(1, feat):
        pl.semaphore_signal(barrier, inc=1, device_id={"feat": lax.rem(me + off, feat)}, device_id_type=pl.DeviceIdType.MESH)
    pl.semaphore_wait(barrier, feat - 1)

    def z_copy(c, off):
        return pltpu.make_async_remote_copy(
            src_ref=zbuf.at[me, c], dst_ref=zbuf.at[me, c], send_sem=z_send.at[c, off - 1], recv_sem=z_recv.at[c, off - 1],
            device_id={"feat": lax.rem(me + off, feat)}, device_id_type=pl.DeviceIdType.MESH)

    def d_copy(off):
        return pltpu.make_async_remote_copy(
            src_ref=dbuf.at[me], dst_ref=dbuf.at[me], send_sem=d_send.at[off - 1], recv_sem=d_recv.at[off - 1],
            device_id={"feat": lax.rem(me + off, feat)}, device_id_type=pl.DeviceIdType.MESH)

    lam = reg_ref[0]
    alpha = step_ref[0]
    lane = lax.broadcasted_iota(jnp.int32, (hid, LANES), 1)

    for j in range(hid // LANES):
        row = w2_ref[j:j + 1, :]
        w2b[j * LANES:(j + 1) * LANES, :] = jnp.transpose(jnp.broadcast_to(row, (LANES, LANES)))
    theta[:, :tail] = w_ref[:, :tail]
    w2_all = w2b[...]
    theta[:, tail:] = jnp.where(lane == tail_n, w2_all, 0.0)
    theta[:, tail:dim] = w_ref[:, tail:]
    for ref in (hist_s, hist_y):
        ref[...] = jnp.zeros_like(ref)
    grad[...] = jnp.zeros_like(grad)
    for g in range(hid // 16):
        sl = slice(16 * g, 16 * g + 16)
        for ref, val in zip(parts_refs, split3(theta[sl, :])):
            ref[sl, :] = val

    row1 = jnp.zeros((8, LANES), F32)

    def iteration(k, carry):
        rho0p, rho1p, sg0p, sg1p, yg0p, yg1p, yy00p, yy01p, yy11p, sy01p = carry
        n0 = lax.rem(k, HIST)
        n1 = lax.rem(k + 2, HIST)
        n2 = lax.rem(k + 1, HIST)
        live = k > 0

        for c in range(n_chunks):
            cols = slice(CHUNK * c, CHUNK * (c + 1))
            act[:, cols] = exact_dot([ref[:, :dim] for ref in parts_refs], x_ref[cols, :], NT)
            acc = jnp.zeros((8, CHUNK), F32)
            for g in range(hid // 8):
                sl = slice(8 * g, 8 * g + 8)
                h = jnp.tanh(act[sl, cols] * in_scale)
                act[sl, cols] = h
                acc = acc + h * jnp.concatenate([w2b[sl, :]] * q_n, axis=1)
            zrow = sub_sum(acc) * out_scale
            for q in range(q_n):
                zbuf[me, c, q:q + 1, :] = zrow[:, LANES * q:LANES * (q + 1)]
            for off in range(1, feat):
                z_copy(c, off).start()

        loss_acc = jnp.zeros((q_n, LANES), F32)
        gcol = [jnp.zeros((16, LANES), F32) for _ in range(hid // 16)]
        for c in range(n_chunks):
            cols = slice(CHUNK * c, CHUNK * (c + 1))
            for off in range(1, feat):
                z_copy(c, off).wait()
            z = zbuf[0, c]
            for src in range(1, feat):
                z = z + zbuf[src, c]
            t = t_ref[c]
            ez = jnp.exp(-jnp.abs(z))
            loss_acc = loss_acc + (jnp.maximum(z, 0.0) + jnp.log1p(ez) - t * z)
            sig = jnp.where(z >= 0.0, 1.0, ez) / (1.0 + ez)
            r = (sig - t) * (1.0 / rows)
            rrow = jnp.concatenate([r[q:q + 1, :] for q in range(q_n)], axis=1)
            rscaled = rrow * (out_scale * in_scale)
            for g in range(hid // 16):
                sl = slice(16 * g, 16 * g + 16)
                h = act[sl, cols]
                w2t = jnp.concatenate([w2b[sl, :]] * q_n, axis=1)
                hr = h * rrow
                s = hr[:, :LANES]
                for q in range(1, q_n):
                    s = s + hr[:, LANES * q:LANES * (q + 1)]
                gcol[g] = gcol[g] + s
                d = rscaled * w2t * (1.0 - h * h)
                for ref, val in zip((d_hi, d_mid, d_lo), split3(d)):
                    ref[c % 2, sl, :] = val
            prod = exact_dot([ref[c % 2] for ref in (d_hi, d_mid, d_lo)], x_ref[cols, :], NN)
            if c == 0:
                hist_y[n0, :, :dim] = prod
            else:
                hist_y[n0, :, :dim] = hist_y[n0, :, :dim] + prod
        loss_ref[k] = jnp.sum(loss_acc) * (1.0 / rows)
        for g in range(hid // 16):
            sl = slice(16 * g, 16 * g + 16)
            hist_y[n0, sl, dim:dim + 1] = jnp.sum(gcol[g], axis=1, keepdims=True) * out_scale

        def dots(i, accs):
            base = pl.multiple_of(i * 16, 16)
            sl = pl.ds(base, 16)
            accs = list(accs)
            for b in range(wide // LANES):
                ln = slice(LANES * b, LANES * (b + 1))
                gk = hist_y[n0, sl, ln] + lam * theta[sl, ln]
                y0 = jnp.where(live, gk - grad[sl, ln], 0.0)
                grad[sl, ln] = gk
                hist_y[n0, sl, ln] = y0
                s0 = hist_s[n0, sl, ln]
                s1 = hist_s[n1, sl, ln]
                s2 = hist_s[n2, sl, ln]
                y1 = hist_y[n1, sl, ln]
                y2 = hist_y[n2, sl, ln]
                for n, (u, v) in enumerate(((s0, gk), (y0, gk), (y0, y0), (y0, y1), (y0, y2), (s0, y0), (s1, y0), (s2, y0))):
                    accs[n] = accs[n] + u * v
            return tuple(accs)

        accs = lax.fori_loop(0, hid // 16, dots, tuple(jnp.zeros((16, LANES), F32) for _ in range(8)))
        for n in range(8):
            dbuf[me, n:n + 1, :] = sub_sum(accs[n])
        for off in range(1, feat):
            d_copy(off).start()
        for off in range(1, feat):
            d_copy(off).wait()
        tot = dbuf[0]
        for src in range(1, feat):
            tot = tot + dbuf[src]
        tot = jnp.broadcast_to(jnp.sum(tot, axis=1, keepdims=True), (8, LANES))
        sg0, yg0, yy00, yy01, yy02, sy00, sy01, sy02 = [jnp.broadcast_to(tot[n:n + 1, :], (8, LANES)) for n in range(8)]
        sg1 = sg0p + sy01
        sg2 = sg1p + sy02
        yg1 = yg0p + yy01
        yg2 = yg1p + yy02
        yy11, yy12, yy22 = yy00p, yy01p, yy11p
        sy12 = sy01p
        rho0 = jnp.where(live, 1.0 / sy00, 0.0)
        gamma = jnp.where(live, sy00 / yy00, 1.0)
        rho1, rho2 = rho0p, rho1p
        a0 = rho0 * sg0
        a1 = rho1 * (sg1 - a0 * sy01)
        a2 = rho2 * (sg2 - a0 * sy02 - a1 * sy12)
        b2 = rho2 * gamma * (yg2 - a0 * yy02 - a1 * yy12 - a2 * yy22)
        e2 = a2 - b2
        b1 = rho1 * (gamma * (yg1 - a0 * yy01 - a1 * yy11 - a2 * yy12) + e2 * sy12)
        e1 = a1 - b1
        b0 = rho0 * (gamma * (yg0 - a0 * yy00 - a1 * yy01 - a2 * yy02) + e2 * sy02 + e1 * sy01)
        e0 = a0 - b0
        coefs = [-alpha * gamma, alpha * gamma * a0, alpha * gamma * a1, alpha * gamma * a2, -alpha * e0, -alpha * e1, -alpha * e2]
        coefs = [jnp.concatenate([v, v], axis=0) for v in coefs]

        def update(i, none):
            base = pl.multiple_of(i * 16, 16)
            sl = pl.ds(base, 16)
            for b in range(wide // LANES):
                ln = slice(LANES * b, LANES * (b + 1))
                old = theta[sl, ln]
                step = coefs[0] * grad[sl, ln]
                for n, (ref, slot) in enumerate(((hist_y, n0), (hist_y, n1), (hist_y, n2), (hist_s, n0), (hist_s, n1), (hist_s, n2))):
                    step = step + coefs[n + 1] * ref[slot, sl, ln]
                new = old + step
                theta[sl, ln] = new
                hist_s[n2, sl, ln] = new - old
                for ref, val in zip(parts_refs, split3(new)):
                    ref[sl, ln] = val
            return none

        lax.fori_loop(0, hid // 16, update, 0)
        w2b[...] = jnp.broadcast_to(theta[:, dim:dim + 1], (hid, LANES))
        return rho0, rho1, sg0, sg1, yg0, yg1, yy00, yy01, yy11, sy01

    lax.fori_loop(0, NUM_ITERS, iteration, tuple(row1 for _ in range(10)))
    wout_ref[...] = theta[:, :dim]
    for j in range(hid // LANES):
        w2out_ref[j:j + 1, :] = jnp.transpose(w2b[j * LANES:(j + 1) * LANES, :])[0:1, :]


def solution(mesh):
    feat = mesh.shape["feat"]

    def local_solve(x_loc, t_loc, win_loc, wout_loc, reg_loc, step_loc):
        rows, dim = x_loc.shape
        hid = win_loc.shape[0]
        wide = (dim // LANES + 1) * LANES
        n_chunks = rows // CHUNK
        q_n = CHUNK // LANES
        vmem = pl.BlockSpec(memory_space=pltpu.VMEM)
        smem = pl.BlockSpec(memory_space=pltpu.SMEM)
        w_new, w2_new, losses = pl.pallas_call(
            functools.partial(kernel, feat),
            out_shape=(jax.ShapeDtypeStruct((hid, dim), F32), jax.ShapeDtypeStruct((hid // LANES, LANES), F32),
                       jax.ShapeDtypeStruct((NUM_ITERS,), F32)),
            in_specs=[smem, smem, vmem, vmem, vmem, vmem],
            out_specs=(vmem, vmem, smem),
            scratch_shapes=[
                pltpu.VMEM((hid, wide), F32), pltpu.VMEM((hid, wide), F32),
                pltpu.VMEM((HIST, hid, wide), F32), pltpu.VMEM((HIST, hid, wide), F32),
                pltpu.VMEM((hid, wide), BF16), pltpu.VMEM((hid, wide), BF16), pltpu.VMEM((hid, wide), BF16),
                pltpu.VMEM((hid, rows), F32), pltpu.VMEM((hid, LANES), F32),
                pltpu.VMEM((2, hid, CHUNK), BF16), pltpu.VMEM((2, hid, CHUNK), BF16), pltpu.VMEM((2, hid, CHUNK), BF16),
                pltpu.VMEM((feat, n_chunks, q_n, LANES), F32), pltpu.VMEM((feat, 8, LANES), F32),
                pltpu.SemaphoreType.DMA((n_chunks, feat - 1)), pltpu.SemaphoreType.DMA((n_chunks, feat - 1)),
                pltpu.SemaphoreType.DMA((feat - 1,)), pltpu.SemaphoreType.DMA((feat - 1,)),
            ],
            compiler_params=pltpu.CompilerParams(collective_id=0, has_side_effects=True),
        )(reg_loc, step_loc, x_loc, t_loc.reshape(n_chunks, q_n, LANES), win_loc, wout_loc.reshape(hid // LANES, LANES))
        return w_new, w2_new.reshape(hid), losses

    specs_in = (P("prob", None), P("prob"), P(("prob", "feat"), None), P(("prob", "feat")), P("prob"), P("prob"))
    specs_out = (P(("prob", "feat"), None), P(("prob", "feat")), P("prob"))
    return jax.shard_map(local_solve, mesh=mesh, in_specs=specs_in, out_specs=specs_out, check_vma=False)
```

time: 464 us -> 102 us (0.22); the launches traced: 457 us -> 102 us
  blocking collectives: 197 us -> 0 us
  matrix products: 90.1 us -> 0 us
  Pallas kernels: 0 us -> 86.7 us
  other arithmetic: 82.8 us -> 0 us
  between operations: 75.5 us -> 1.93 us
    psum x30 -> x0, blocking collectives: 197 us -> none  [the longest x19 124 us: global_dot(): return lax.psum(pair_dot_local(first, second), 'feat')]
    dot_general x24 -> x0, matrix products: 90.1 us -> none  [the longest x6 43.1 us: local_solve(): lax.dot_general(d_pre, x_f32, (((0,), (0,)), ((), ())), precision=FULL_PREC)]
    pallas_call x0 -> x1, Pallas kernels: none -> 86.7 us  [local_solve(): pl.pallas_call(functools.partial(kernel, feat), out_shape=(jax.ShapeDtype...]
    reduce_sum x44 -> x0, other arithmetic: 70.2 us -> none  [the longest x43 69.5 us: pair_dot_local(): return jnp.sum(first[0] * second[0]) + jnp.sum(first[1] * second[1])]
    add x6 -> x0, other arithmetic: 12.1 us -> none  [pair_axpy(): return (base[0] + coef * other[0], base[1] + coef * other[1])]
    unnamed x40 -> x5, local copies, waits for them, and re-layouts: 8.38 us -> 13 us
where the time goes in v1:
time: 102 us
  Pallas kernels  86.7 us (85%)
  local copies, waits for them, and re-layouts  13 us (13%)
  between operations  1.93 us (2%)
    pallas_call x1, Pallas kernels, local_solve(): pl.pallas_call(functools.partial(kernel, feat), out_shape=(jax.ShapeDtype...  86.7 us
    unnamed x5, local copies, waits for them, and re-layouts  13 us

profile of v1, /device:TPU:0, one launch (start us, length us, event | category | flops | bytes accessed | tf_op | source)
XLA Modules:
  0.0 101.6 jit_solution(16468156831246406622)
XLA Ops:
  1.9 2.4 %copy.10.w_ref = f32[256,784]{1,0:T(8,128)} copy(f32[256,784]{0,1:T(8,128)} %param.8) | data formatting | bytes 1605632 | tf_op args[2]
  4.3 6.0 %copy.9.x_ref = bf16[2048,784]{1,0:T(8,128)(2,1)} copy(bf16[2048,784]{0,1:T(8,128)(2,1)} %param.6) | data formatting | bytes 6422528 | tf_op args[0]
  10.3 86.7 %shard_map.85 = (f32[256,784]{1,0:T(8,128)}, f32[2,128]{1,0:T(2,128)}, f32[6]{0:T(128)}) custom-call(f32[1]{0:T(128)S(6)} %copy.14.reg_ref, f32[1]{0:T(128)S(6)} %copy.15.step_ref, bf16[2048,784]{1,0:T(8,128)(2,1)} %copy.9.x_ref, f32[4,4,128]{2,1,0:T(4,128)} %bitcast.3, f32[256,784]{1,0:T(8,128)} %copy.10.w_ref, f32[2,128]{1,0:T(2,128)} %bitcast.5), custom_call_target="tpu_custom_call" | custom-call | tf_op jit(solution)/shard_map/pallas_call | solution.py:240
  96.9 2.3 %copy.11 = f32[256,784]{0,1:T(8,128)} copy(f32[256,784]{1,0:T(8,128)} %get-tuple-element.9) | data formatting | bytes 1605632
  99.3 1.2 %copy.16 = f32[256]{0:T(256)} copy(f32[256]{0:T(256)} %bitcast.4) | data formatting | bytes 2048
  100.5 1.1 %copy.17 = f32[6]{0:T(128)} copy(f32[6]{0:T(128)} %get-tuple-element.17) | data formatting | bytes 48
